TPU v7x, 128 devices: a whole 4x4x4 slice. The times are simulated.
128 devices in a mesh: seq: 16 (over z_hi, y, core), head: 8 (over x, z_lo).
Axes of the slice: x: 4, y: 4, z: 4 (z_hi: 2, z_lo: 2; z = z_hi * 2 + z_lo), core: 2. Of those that a mesh axis runs over, the one named last changes fastest.
Arguments:
- latent: bfloat16 [16, 1024, 2048], P('seq', None, 'head'), may hold values from -6 to 6
- modulation: float32 [9, 2048], replicated, may hold values from -3 to 3
- spatial_qkv: bfloat16 [3, 2048, 2048], P(None, None, 'head')
- spatial_out: bfloat16 [2048, 2048], P('head'), may hold values from -0.125 to 0.125
- temporal_qkv: bfloat16 [3, 2048, 2048], P(None, None, 'head')
- temporal_out: bfloat16 [2048, 2048], P('head'), may hold values from -0.125 to 0.125
- hidden_weight: bfloat16 [2048, 8192], P(None, 'head'), may hold values from -0.125 to 0.125
- output_weight: bfloat16 [8192, 2048], P('head'), may hold values from -0.0625 to 0.0625
Outputs:
- block_out: bfloat16 [16, 1024, 2048], P(None, 'seq', 'head')
All inputs are finite; a program needn't handle non-finite values.
Results may differ from a plain program's by a relative error of at most 0.009.
Values may be sent and summed in bfloat16 or wider, within the bound.
A program may use at most 128 MiB of HBM per device.

v0:
```python
import jax
import jax.numpy as jnp
from jax import lax
from jax.sharding import PartitionSpec as P

HD = 64


def split_up(shard, dim, devices):
    lengths = shard.shape
    blocks = shard.reshape(*lengths[:dim], devices, lengths[dim] // devices, *lengths[dim + 1 :])
    return jnp.moveaxis(blocks, dim, 0)


def sum_at_owner(shard, axis, dim):
    devices = lax.axis_size(axis)
    blocks = lax.all_to_all(split_up(shard, dim, devices), axis, 0, 0, tiled=True)
    return jnp.sum(blocks.astype(jnp.float32), axis=0)


def layer_norm(values):
    average = jnp.mean(values, axis=-1, keepdims=True)
    centred = values - average
    variance = jnp.mean(centred * centred, axis=-1, keepdims=True)
    return centred * lax.rsqrt(variance + 1e-06)


def modulate(stream, modulation, offset):
    normed = layer_norm(stream.astype(jnp.float32))
    return (normed * (1.0 + modulation[offset + 1]) + modulation[offset]).astype(jnp.bfloat16)


def attend(query, keys, values):
    scores = jnp.einsum(
        "glhd,gmhd->ghlm", query, keys, preferred_element_type=jnp.float32
    ) * HD ** (-0.5)
    attn_weights = jax.nn.softmax(scores, axis=-1).astype(jnp.bfloat16)
    return jnp.einsum(
        "ghlm,gmhd->glhd", attn_weights, values, preferred_element_type=jnp.float32
    ).astype(jnp.bfloat16)


def project_three(normed, weights):
    return [
        jnp.dot(normed, weights[member], preferred_element_type=jnp.float32).astype(jnp.bfloat16)
        for member in range(3)
    ]


def column_adder(columns, portion):
    return jnp.dot(portion, columns, preferred_element_type=jnp.float32)


def per_device(
    latent,
    modulation,
    spatial_qkv,
    spatial_out,
    temporal_qkv,
    temporal_out,
    hidden_weight,
    output_weight,
):
    width_local = latent.shape[2]
    heads_local = width_local // HD
    anchor = lax.axis_index("head") * width_local
    local_rows = lax.dynamic_slice_in_dim(modulation, anchor, width_local, 1)
    full_spatial = lax.all_gather(latent, "head", axis=2, tiled=True)
    normed = modulate(full_spatial, modulation, 0)
    frames_local = latent.shape[0]
    patches = latent.shape[1]
    query, keys, values = [
        member.reshape(frames_local, patches, heads_local, HD)
        for member in project_three(normed, spatial_qkv)
    ]
    spatial = lax.map(
        lambda triple: attend(triple[0][None], triple[1][None], triple[2][None])[0],
        (query, keys, values),
    )
    spatial = spatial.reshape(frames_local, patches, width_local)
    columns = lax.all_to_all(spatial_out, "head", split_axis=1, concat_axis=0, tiled=True)
    reduced = column_adder(columns, lax.all_gather(spatial, "head", axis=2, tiled=True))
    stream_one = (latent.astype(jnp.float32) + local_rows[2] * reduced).astype(jnp.bfloat16)
    stream_temporal = lax.all_to_all(stream_one, "seq", split_axis=1, concat_axis=0, tiled=True)
    full_temporal = lax.all_gather(stream_temporal, "head", axis=2, tiled=True)
    normed = modulate(full_temporal, modulation, 3)
    query, keys, values = project_three(normed, temporal_qkv)
    frames = stream_temporal.shape[0]
    patches_local = stream_temporal.shape[1]

    def to_groups(tensor):
        return jnp.transpose(tensor.reshape(frames, patches_local, heads_local, HD), (1, 0, 2, 3))

    temporal = attend(to_groups(query), to_groups(keys), to_groups(values))
    temporal = jnp.transpose(temporal, (1, 0, 2, 3)).reshape(frames, patches_local, width_local)
    columns = lax.all_to_all(temporal_out, "head", split_axis=1, concat_axis=0, tiled=True)
    reduced = column_adder(columns, lax.all_gather(temporal, "head", axis=2, tiled=True))
    stream_two = (stream_temporal.astype(jnp.float32) + local_rows[5] * reduced).astype(
        jnp.bfloat16
    )
    full_two = lax.all_gather(stream_two, "head", axis=2, tiled=True)
    normed = modulate(full_two, modulation, 6)
    pre_act = jnp.dot(normed, hidden_weight, preferred_element_type=jnp.float32)
    hidden = jax.nn.gelu(pre_act, approximate=True).astype(jnp.bfloat16)
    partial_sums = jnp.dot(hidden, output_weight, preferred_element_type=jnp.float32)
    reduced = sum_at_owner(partial_sums.astype(jnp.bfloat16), "head", 2)
    return (stream_two.astype(jnp.float32) + local_rows[8] * reduced).astype(jnp.bfloat16)


def solution(mesh):
    in_specs = (
        P("seq", None, "head"),
        P(),
        P(None, None, "head"),
        P("head", None),
        P(None, None, "head"),
        P("head", None),
        P(None, "head"),
        P("head", None),
    )
    out_specs = P(None, "seq", "head")
    return jax.shard_map(
        per_device, mesh=mesh, in_specs=in_specs, out_specs=out_specs, check_vma=False
    )
```

profile of v0, /device:TPU:8, one launch (start us, length us, event | category | flops | bytes accessed | tf_op | source)
XLA Modules:
  0.0 685.8 jit_solution(7628114898617417352)
XLA Ops:
  8.4 99.1 %all-gather.6.cloned.1.call-done = bf16[1,1024,2048]{2,1,0:T(8,128)(2,1)} async-done(((bf16[1,1024,256]{2,1,0:T(8,128)(2,1)}), bf16[1,1024,2048]{2,1,0:T(8,128)(2,1)}) %all-gather.6.cloned.1.call-update) | async-done | bytes 4194320 | tf_op jit(solution)/shard_map/all_gather | solution.py:68
  107.6 3.0 convert_reduce_fusion.2
  118.1 5.2 fusion.130
  123.3 8.1 %fusion.136 = f32[4,1024,1024]{1,2,0:T(8,128)} fusion(bf16[1024,4,64]{0,2,1:T(8,128)(2,1)S(1)} %bitcast.142, bf16[1024,4,64]{0,2,1:T(8,128)(2,1)S(1)} %bitcast.144), kind=kOutput, calls=%fused_computation.124 | convolution fusion | flops 536870912 | bytes 17825792 | tf_op jit(solution)/shard_map/while/body/eval_jaxpr/glhd,gmhd->ghlm/dot_general | solution.py:34
  131.4 16.0 %fusion.69 = bf16[4,64,1024]{2,1,0:T(8,128)(2,1)} fusion(bf16[1024,4,64]{0,2,1:T(8,128)(2,1)S(1)} %bitcast.162, f32[4,1024]{1,0:T(4,128)S(1)} %fusion.130, f32[4,1024,1024]{1,2,0:T(8,128)} %fusion.136), kind=kOutput, calls=%fused_computation.78 | convolution fusion | flops 558109696 | bytes 17842176 | tf_op jit(solution)/shard_map/while/body/eval_jaxpr/ghlm,gmhd->glhd/dot_general | solution.py:38
  148.7 6.0 all-to-all-start
  155.6 21.3 %all-to-all-done = bf16[256,8,256]{0,2,1:T(8,128)(2,1)S(1)} async-done(((bf16[256,8,256]{0,2,1:T(8,128)(2,1)}), bf16[256,8,256]{0,2,1:T(8,128)(2,1)S(1)}, u32[]{:S(2)}, u32[]{:S(2)}) %all-to-all-start) | async-done | bytes 1048608 | tf_op jit(solution)/shard_map/all_to_all | solution.py:81
  177.5 71.1 %all-gather.8.cloned.1.call-done = bf16[1,1024,2048]{1,2,0:T(8,128)(2,1)} async-done(((bf16[1,1024,256]{1,2,0:T(8,128)(2,1)}), bf16[1,1024,2048]{1,2,0:T(8,128)(2,1)}) %all-gather.8.cloned.1.call-update) | async-done | bytes 4194320 | tf_op jit(solution)/shard_map/all_gather | solution.py:82
  248.6 3.5 fusion.65
  253.4 3.8 reduce.6
  257.4 15.9 %all_to_all.55 = bf16[16,2,8192]{2,1,0:T(2,128)(2,1)S(1)} all-to-all(bf16[16,2,8192]{2,1,0:T(2,128)(2,1)S(1)} %reshape.181), channel_id=1, replica_groups=mesh['seq'=16,'head'=8] {'seq'}, dimensions={0} | all-to-all | bytes 1048576 | tf_op jit(solution)/shard_map/all_to_all | solution.py:84
  274.9 94.6 %all-gather.10.cloned.1.call-done = bf16[16,64,2048]{2,1,0:T(8,128)(2,1)} async-done(((bf16[16,64,256]{2,1,0:T(8,128)(2,1)}), bf16[16,64,2048]{2,1,0:T(8,128)(2,1)}) %all-gather.10.cloned.1.call-update) | async-done | bytes 4194320 | tf_op jit(solution)/shard_map/all_gather | solution.py:85
  369.5 3.0 convert_reduce_fusion.1
  374.2 3.0 convolution_convert_fusion.1
  377.5 4.2 convolution_convert_fusion.2
  382.2 5.0 convolution_convert_fusion.3
  389.4 3.3 fusion.131
  397.4 24.8 %all_to_all.56 = bf16[256,8,256]{2,0,1:T(8,128)(2,1)S(1)} all-to-all(bf16[256,8,256]{2,0,1:T(8,128)(2,1)S(1)} %bitcast.138), channel_id=1, replica_groups=mesh['seq'=16,'head'=8] {'head'}, dimensions={1} | all-to-all | bytes 2097152 | tf_op jit(solution)/shard_map/all_to_all | solution.py:96
  422.2 74.8 %all-gather.12.cloned.1.call-done = bf16[16,64,2048]{2,1,0:T(8,128)(2,1)} async-done(((bf16[16,64,256]{2,1,0:T(8,128)(2,1)}), bf16[16,64,2048]{2,1,0:T(8,128)(2,1)}) %all-gather.12.cloned.1.call-update) | async-done | bytes 4194320 | tf_op jit(solution)/shard_map/all_gather | solution.py:97
  497.0 4.2 fusion.68
  501.3 100.4 %all-gather.14.cloned.1.call-done = bf16[16,64,2048]{2,1,0:T(8,128)(2,1)} async-done(((bf16[16,64,256]{2,1,0:T(8,128)(2,1)}), bf16[16,64,2048]{2,1,0:T(8,128)(2,1)}) %all-gather.14.cloned.1.call-update) | async-done | bytes 4194320 | tf_op jit(solution)/shard_map/all_gather | solution.py:101
  601.7 3.0 convert_reduce_fusion
  606.4 15.3 %fusion.45 = bf16[16,64,2048]{2,1,0:T(8,128)(2,1)} fusion(bf16[1024,2048]{1,0:T(8,128)(2,1)} %param.15, bf16[16,64,2048]{2,1,0:T(8,128)(2,1)} %all-gather.14.cloned.1.call-done, bf16[2048,1024]{1,0:T(8,128)(2,1)} %param.14, f32[2048]{0:T(1024)S(1)} %bitcast.152, f32[2048]{0:T(1024)S(1)} %bitcast.151, f32[16,64]{1,0:T(8,128)S(1)} %add_rsqrt_fusion, ...), kind=kOutput, calls=%fused_computation.54 | convolution fusion | flops 8614051840 | bytes 16801792 | tf_op jit(solution)/shard_map/dot_general | solution.py:105
  624.5 52.6 %all_to_all.57 = bf16[8,16,64,256]{3,2,1,0:T(8,128)(2,1)S(1)} all-to-all(bf16[8,16,64,256]{3,2,1,0:T(8,128)(2,1)S(1)} %bitcast.133), channel_id=1, replica_groups=mesh['seq'=16,'head'=8] {'head'}, dimensions={0} | all-to-all | bytes 8388608 | tf_op jit(solution)/shard_map/all_to_all | solution.py:17
  (60 shorter events, 31.0 us)
Async XLA Ops:
  6.5 101.0 %all-gather.6.cloned.1.call-start = ((), (), s32[]{:S(2)}) async-start(), calls=%async_computation.4 | async-start | bytes 4718592 | tf_op jit(solution)/shard_map/all_gather | solution.py:68
  7.3 241.3 %all-gather.8.cloned.1.call-start = ((), (), s32[]{:S(2)}) async-start(), calls=%async_computation.5 | async-start | bytes 4718592 | tf_op jit(solution)/shard_map/all_gather | solution.py:82
  107.6 3.4 copy-start
  112.3 1.9 copy-start.8
  131.4 16.0 %copy-start.5 = (bf16[256,2048]{1,0:T(8,128)(2,1)S(1)}, bf16[256,2048]{1,0:T(8,128)(2,1)}, u32[]{:S(2)}) copy-start(bf16[256,2048]{1,0:T(8,128)(2,1)} %param.11) | copy-start | bytes 3145732
  147.4 101.2 %copy-start.7 = (bf16[1,1024,256]{2,1,0:T(8,128)(2,1)S(1)}, bf16[1,1024,256]{2,1,0:T(8,128)(2,1)}, u32[]{:S(2)}) copy-start(bf16[1,1024,256]{2,1,0:T(8,128)(2,1)} %param.8) | copy-start | bytes 1572868
  148.7 28.2 %all-to-all-start = ((bf16[256,8,256]{0,2,1:T(8,128)(2,1)}), bf16[256,8,256]{0,2,1:T(8,128)(2,1)S(1)}, u32[]{:S(2)}, u32[]{:S(2)}) async-start(bf16[256,8,256]{0,2,1:T(8,128)(2,1)} %bitcast.14), calls=%async_computation | async-start | bytes 2097152 | tf_op jit(solution)/shard_map/all_to_all | solution.py:81
  154.7 214.7 %all-gather.10.cloned.1.call-start = ((), (), s32[]{:S(2)}) async-start(), calls=%async_computation.6 | async-start | bytes 4718592 | tf_op jit(solution)/shard_map/all_gather | solution.py:85
  274.7 222.4 %all-gather.12.cloned.1.call-start = ((), (), s32[]{:S(2)}) async-start(), calls=%async_computation.7 | async-start | bytes 4718592 | tf_op jit(solution)/shard_map/all_gather | solution.py:97
  369.5 3.4 copy-start.1
  395.2 2.1 copy-start.6
  395.2 101.8 %copy-start.3 = (bf16[1,1024,256]{2,1,0:T(8,128)(2,1)S(1)}, bf16[1,1024,256]{2,1,0:T(8,128)(2,1)}, u32[]{:S(2)}) copy-start(bf16[1,1024,256]{2,1,0:T(8,128)(2,1)} %copy.55) | copy-start | bytes 1572868
  397.2 204.5 %all-gather.14.cloned.1.call-start = ((), (), s32[]{:S(2)}) async-start(), calls=%async_computation.8 | async-start | bytes 4718592 | tf_op jit(solution)/shard_map/all_gather | solution.py:101
  601.7 3.4 copy-start.2
  677.1 1.0 copy-start.4
Sparse Core Ops, SparseCore 0:
  8.9 98.6 all-gather.5
  147.5 101.0 all-gather.7
  274.8 94.6 all-gather.9
  397.3 99.6 all-gather.11
  501.4 100.2 all-gather.13
where the time goes:
time: 696 us; the launch traced here: 686 us
  waiting for transfers between devices  462 us (66%)
  blocking collectives  93.3 us (13%)
  matrix products  74.2 us (11%)
  other arithmetic  21.1 us (3%)
  local copies, waits for them, and re-layouts  15.2 us (2%)
  between operations  13.6 us (2%)
    all_gather x1, waiting for transfers between devices, per_device(): full_two = lax.all_gather(stream_two, 'head', axis=2, tiled=True)  100 us
    all_gather x1, waiting for transfers between devices, per_device(): full_spatial = lax.all_gather(latent, 'head', axis=2, tiled=True)  99.1 us
    all_gather x1, waiting for transfers between devices, per_device(): full_temporal = lax.all_gather(stream_temporal, 'head', axis=2, tiled=True)  94.6 us
    all_gather x1, waiting for transfers between devices, per_device(): lax.all_gather(temporal, 'head', axis=2, tiled=True)  74.8 us
    all_gather x1, waiting for transfers between devices, per_device(): lax.all_gather(spatial, 'head', axis=2, tiled=True)  71.1 us
    all_to_all x1, blocking collectives, sum_at_owner(): lax.all_to_all(split_up(shard, dim, devices), axis, 0, 0, tiled=True)  52.6 us
    all_to_all x1, blocking collectives, per_device(): lax.all_to_all(temporal_out, 'head', split_axis=1, concat_axis=0, tiled=T...  24.8 us
    all_to_all x1, waiting for transfers between devices, per_device(): lax.all_to_all(spatial_out, 'head', split_axis=1, concat_axis=0, tiled=True)  21.3 us
  transfers between devices with their start and end apart: 6, of which 6 were waited for; matrix products, arithmetic and copies ran while one was open for 1% of the time, Pallas kernels for 0%

commit v1 on v0

--- a/solution.py
+++ b/solution.py
@@ -65,7 +65,9 @@
     heads_local = width_local // HD
     anchor = lax.axis_index("head") * width_local
     local_rows = lax.dynamic_slice_in_dim(modulation, anchor, width_local, 1)
-    full_spatial = lax.all_gather(latent, "head", axis=2, tiled=True)
+    full_spatial = jnp.concatenate(
+        lax.all_to_all(jnp.stack([latent] * lax.axis_size("head")), "head", 0, 0), axis=2
+    )
     normed = modulate(full_spatial, modulation, 0)
     frames_local = latent.shape[0]
     patches = latent.shape[1]

time: 696 us -> 660 us (0.948)
  waiting for transfers between devices: 462 us -> 420 us
    all_gather x1 -> x0, waiting for transfers between devices: 99.1 us -> none  [per_device(): full_spatial = lax.all_gather(latent, 'head', axis=2, tiled=True)]
    all_to_all x0 -> x1, waiting for transfers between devices: none -> 58.4 us  [per_device(): lax.all_to_all(jnp.stack([latent] * lax.axis_size('head')), 'head', 0, 0)]
where the time goes in v1:
time: 660 us; the launch traced here: 656 us
  waiting for transfers between devices  420 us (64%)
  blocking collectives  93.8 us (14%)
  matrix products  74.2 us (11%)
  other arithmetic  25.7 us (4%)
  local copies, waits for them, and re-layouts  18.9 us (3%)
  between operations  13.7 us (2%)
  starting transfers between devices  9.54 us (1%)
    all_gather x1, waiting for transfers between devices, per_device(): full_two = lax.all_gather(stream_two, 'head', axis=2, tiled=True)  100 us
    all_gather x1, waiting for transfers between devices, per_device(): full_temporal = lax.all_gather(stream_temporal, 'head', axis=2, tiled=True)  95.9 us
    all_gather x1, waiting for transfers between devices, per_device(): lax.all_gather(temporal, 'head', axis=2, tiled=True)  74.8 us
    all_gather x1, waiting for transfers between devices, per_device(): lax.all_gather(spatial, 'head', axis=2, tiled=True)  71.8 us
    all_to_all x1, waiting for transfers between devices, per_device(): lax.all_to_all(jnp.stack([latent] * lax.axis_size('head')), 'head', 0, 0)  58.4 us
    all_to_all x1, blocking collectives, sum_at_owner(): lax.all_to_all(split_up(shard, dim, devices), axis, 0, 0, tiled=True)  52.6 us
    all_to_all x1, blocking collectives, per_device(): lax.all_to_all(temporal_out, 'head', split_axis=1, concat_axis=0, tiled=T...  24.9 us
    all_to_all x1, waiting for transfers between devices, per_device(): lax.all_to_all(spatial_out, 'head', split_axis=1, concat_axis=0, tiled=True)  19 us
  transfers between devices with their start and end apart: 6, of which 6 were waited for; matrix products, arithmetic and copies ran while one was open for 1% of the time, Pallas kernels for 0%

profile of v1, /device:TPU:8, one launch (start us, length us, event | category | flops | bytes accessed | tf_op | source)
XLA Modules:
  0.0 656.3 jit_solution(14974057974837063321)
XLA Ops:
  10.3 5.7 all-to-all-start
  17.2 58.4 %all-to-all-done = bf16[8,1,1024,256]{2,3,1,0:T(8,128)(2,1)} async-done(((bf16[8,1,1024,256]{2,3,1,0:T(8,128)(2,1)}), bf16[8,1,1024,256]{2,3,1,0:T(8,128)(2,1)}, u32[]{:S(2)}, u32[]{:S(2)}) %all-to-all-start) | async-done | bytes 4194336 | tf_op jit(solution)/shard_map/all_to_all | solution.py:69
  78.4 3.2 bitcast_convert_fusion
  82.6 3.7 add_convert_fusion
  90.2 5.2 fusion.126
  95.5 8.1 %fusion.132 = f32[4,1024,1024]{1,2,0:T(8,128)} fusion(bf16[1024,4,64]{0,2,1:T(8,128)(2,1)S(1)} %bitcast.159, bf16[1024,4,64]{0,2,1:T(8,128)(2,1)S(1)} %bitcast.161), kind=kOutput, calls=%fused_computation.122 | convolution fusion | flops 536870912 | bytes 17825792 | tf_op jit(solution)/shard_map/while/body/eval_jaxpr/glhd,gmhd->ghlm/dot_general | solution.py:34
  103.5 16.0 %fusion.65 = bf16[4,64,1024]{2,1,0:T(8,128)(2,1)} fusion(bf16[1024,4,64]{0,2,1:T(8,128)(2,1)S(1)} %bitcast.178, f32[4,1024]{1,0:T(4,128)S(1)} %fusion.126, f32[4,1024,1024]{1,2,0:T(8,128)} %fusion.132), kind=kOutput, calls=%fused_computation.75 | convolution fusion | flops 558109696 | bytes 17842176 | tf_op jit(solution)/shard_map/while/body/eval_jaxpr/ghlm,gmhd->glhd/dot_general | solution.py:38
  120.9 3.6 all-to-all-start.1
  125.4 19.0 %all-to-all-done.1 = bf16[256,8,256]{0,2,1:T(8,128)(2,1)S(1)} async-done(((bf16[256,8,256]{0,2,1:T(8,128)(2,1)}), bf16[256,8,256]{0,2,1:T(8,128)(2,1)S(1)}, u32[]{:S(2)}, u32[]{:S(2)}) %all-to-all-start.1) | async-done | bytes 1048608 | tf_op jit(solution)/shard_map/all_to_all | solution.py:83
  145.4 71.8 %all-gather.5.cloned.1.call-done = bf16[1,1024,2048]{1,2,0:T(8,128)(2,1)} async-done(((bf16[1,1024,256]{1,2,0:T(8,128)(2,1)}), bf16[1,1024,2048]{1,2,0:T(8,128)(2,1)}) %all-gather.5.cloned.1.call-update) | async-done | bytes 4194320 | tf_op jit(solution)/shard_map/all_gather | solution.py:84
  217.2 3.5 fusion.61
  222.1 3.8 reduce.16
  226.0 16.4 %all_to_all.60 = bf16[16,2,8192]{2,1,0:T(2,128)(2,1)S(1)} all-to-all(bf16[16,2,8192]{2,1,0:T(2,128)(2,1)S(1)} %reshape.373), channel_id=1, replica_groups=mesh['seq'=16,'head'=8] {'seq'}, dimensions={0} | all-to-all | bytes 1048576 | tf_op jit(solution)/shard_map/all_to_all | solution.py:86
  244.0 95.9 %all-gather.7.cloned.1.call-done = bf16[16,64,2048]{2,1,0:T(8,128)(2,1)} async-done(((bf16[16,64,256]{2,1,0:T(8,128)(2,1)}), bf16[16,64,2048]{2,1,0:T(8,128)(2,1)}) %all-gather.7.cloned.1.call-update) | async-done | bytes 4194320 | tf_op jit(solution)/shard_map/all_gather | solution.py:87
  340.0 3.0 convert_reduce_fusion.1
  348.0 4.2 convolution_convert_fusion.2
  352.7 5.0 convolution_convert_fusion.3
  359.9 3.3 fusion.127
  367.8 24.9 %all_to_all.61 = bf16[256,8,256]{2,0,1:T(8,128)(2,1)S(1)} all-to-all(bf16[256,8,256]{2,0,1:T(8,128)(2,1)S(1)} %bitcast.155), channel_id=1, replica_groups=mesh['seq'=16,'head'=8] {'head'}, dimensions={1} | all-to-all | bytes 2097152 | tf_op jit(solution)/shard_map/all_to_all | solution.py:98
  392.7 74.8 %all-gather.9.cloned.1.call-done = bf16[16,64,2048]{2,1,0:T(8,128)(2,1)} async-done(((bf16[16,64,256]{2,1,0:T(8,128)(2,1)}), bf16[16,64,2048]{2,1,0:T(8,128)(2,1)}) %all-gather.9.cloned.1.call-update) | async-done | bytes 4194320 | tf_op jit(solution)/shard_map/all_gather | solution.py:99
  467.5 4.2 fusion.64
  471.8 100.4 %all-gather.11.cloned.1.call-done = bf16[16,64,2048]{2,1,0:T(8,128)(2,1)} async-done(((bf16[16,64,256]{2,1,0:T(8,128)(2,1)}), bf16[16,64,2048]{2,1,0:T(8,128)(2,1)}) %all-gather.11.cloned.1.call-update) | async-done | bytes 4194320 | tf_op jit(solution)/shard_map/all_gather | solution.py:103
  576.9 15.3 %fusion.41 = bf16[16,64,2048]{2,1,0:T(8,128)(2,1)} fusion(bf16[1024,2048]{1,0:T(8,128)(2,1)} %param.15, bf16[16,64,2048]{2,1,0:T(8,128)(2,1)} %all-gather.11.cloned.1.call-done, bf16[2048,1024]{1,0:T(8,128)(2,1)} %param.14, f32[2048]{0:T(1024)S(1)} %bitcast.168, f32[2048]{0:T(1024)S(1)} %bitcast.167, f32[16,64]{1,0:T(8,128)S(1)} %add_rsqrt_fusion, ...), kind=kOutput, calls=%fused_computation.51 | convolution fusion | flops 8614051840 | bytes 16801792 | tf_op jit(solution)/shard_map/dot_general | solution.py:107
  595.0 52.6 %all_to_all.62 = bf16[8,16,64,256]{3,2,1,0:T(8,128)(2,1)S(1)} all-to-all(bf16[8,16,64,256]{3,2,1,0:T(8,128)(2,1)S(1)} %bitcast.147), channel_id=1, replica_groups=mesh['seq'=16,'head'=8] {'head'}, dimensions={0} | all-to-all | bytes 8388608 | tf_op jit(solution)/shard_map/all_to_all | solution.py:17
  (62 shorter events, 40.8 us)
Async XLA Ops:
  10.3 65.3 %all-to-all-start = ((bf16[8,1,1024,256]{2,3,1,0:T(8,128)(2,1)}), bf16[8,1,1024,256]{2,3,1,0:T(8,128)(2,1)}, u32[]{:S(2)}, u32[]{:S(2)}) async-start(bf16[8,1,1024,256]{2,3,1,0:T(8,128)(2,1)} %stack.2), calls=%async_computation | async-start | bytes 8388608 | tf_op jit(solution)/shard_map/all_to_all | solution.py:69
  15.9 201.3 %all-gather.5.cloned.1.call-start = ((), (), s32[]{:S(2)}) async-start(), calls=%async_computation.5 | async-start | bytes 4718592 | tf_op jit(solution)/shard_map/all_gather | solution.py:84
  82.6 3.7 copy-start.7
  103.5 16.0 %copy-start.4 = (bf16[256,2048]{1,0:T(8,128)(2,1)S(1)}, bf16[256,2048]{1,0:T(8,128)(2,1)}, u32[]{:S(2)}) copy-start(bf16[256,2048]{1,0:T(8,128)(2,1)} %param.11) | copy-start | bytes 3145732
  119.5 97.7 %copy-start.6 = (bf16[1,1024,256]{2,1,0:T(8,128)(2,1)S(1)}, bf16[1,1024,256]{2,1,0:T(8,128)(2,1)}, u32[]{:S(2)}) copy-start(bf16[1,1024,256]{2,1,0:T(8,128)(2,1)} %param.8) | copy-start | bytes 1572868
  120.9 23.5 %all-to-all-start.1 = ((bf16[256,8,256]{0,2,1:T(8,128)(2,1)}), bf16[256,8,256]{0,2,1:T(8,128)(2,1)S(1)}, u32[]{:S(2)}, u32[]{:S(2)}) async-start(bf16[256,8,256]{0,2,1:T(8,128)(2,1)} %bitcast.18), calls=%async_computation.1 | async-start | bytes 2097152 | tf_op jit(solution)/shard_map/all_to_all | solution.py:83
  124.5 215.5 %all-gather.7.cloned.1.call-start = ((), (), s32[]{:S(2)}) async-start(), calls=%async_computation.6 | async-start | bytes 4718592 | tf_op jit(solution)/shard_map/all_gather | solution.py:87
  243.8 223.7 %all-gather.9.cloned.1.call-start = ((), (), s32[]{:S(2)}) async-start(), calls=%async_computation.7 | async-start | bytes 4718592 | tf_op jit(solution)/shard_map/all_gather | solution.py:99
  340.0 3.4 copy-start
  365.7 2.1 copy-start.5
  365.7 101.8 %copy-start.2 = (bf16[1,1024,256]{2,1,0:T(8,128)(2,1)S(1)}, bf16[1,1024,256]{2,1,0:T(8,128)(2,1)}, u32[]{:S(2)}) copy-start(bf16[1,1024,256]{2,1,0:T(8,128)(2,1)} %copy.61) | copy-start | bytes 1572868
  367.7 204.5 %all-gather.11.cloned.1.call-start = ((), (), s32[]{:S(2)}) async-start(), calls=%async_computation.8 | async-start | bytes 4718592 | tf_op jit(solution)/shard_map/all_gather | solution.py:103
  572.2 3.4 copy-start.1
  647.5 1.0 copy-start.3
Sparse Core Ops, SparseCore 0:
  119.7 97.5 all-gather.4
  243.9 95.9 all-gather.6
  367.8 99.6 all-gather.8
  471.9 100.2 all-gather.10
